TPU v7x, 256 devices: a whole 4x4x8 slice. The times are simulated.
256 devices in a mesh: vert: 16 (over x, y), feat: 16 (over z, core).
Axes of the slice: x: 4, y: 4, z: 8, core: 2. Of those that a mesh axis runs over, the one named last changes fastest.
Arguments:
- features: bfloat16 [131072, 256], P('vert', 'feat'), may hold values from -6 to 6
- tiles: bfloat16 [1024, 16, 128, 128], P('vert'), may hold values from -0.1875 to 0.1875
- tile_cols: int32 [1024, 16], P('vert'), may hold values from 0 to 127
- tile_count: int32 [1024], P('vert'), may hold values from 1 to 16, as said below
- send_list: int32 [16, 16, 4], P('vert'), may hold values from 0 to 63
- weight: bfloat16 [256, 256], replicated, may hold values from -0.375 to 0.375
- bias: float32 [256], replicated, may hold values from -3 to 3
Outputs:
- node_out: bfloat16 [131072, 256], P(('vert', 'feat'))
Inputs may be any that keep to these rules, and one draw needn't show every extreme that they name: Row block r uses tile places 0 to tile_count[r] - 1; in every draw some row block uses all 16.
All inputs are finite; a program needn't handle non-finite values.
Results may differ from a plain program's by a relative error of at most 0.0044.
Values may be sent and summed in bfloat16 or wider, within the bound.
A program may use at most 128 MiB of HBM per device.

v0:
```python
import jax
import jax.numpy as jnp
from jax import lax
from jax.sharding import PartitionSpec as P


def add_tile(total, extended, tiles, tile_cols, tile_count, tile_slot):
    wanted = lax.dynamic_index_in_dim(tile_cols, tile_slot, 1, keepdims=False)
    picked = jnp.take(extended, wanted, axis=0)
    tile_page = lax.dynamic_index_in_dim(tiles, tile_slot, 1, keepdims=False)
    product = jnp.einsum("rcj,rij->cri", picked, tile_page, preferred_element_type=jnp.float32)
    is_live = tile_slot < tile_count
    return total + jnp.where(is_live[None, :, None], product, jnp.float32(0.0))


def per_device(features, tiles, tile_cols, tile_count, send_list, weight, bias):
    block_count = tiles.shape[0]
    tile_depth = tiles.shape[1]
    edge = tiles.shape[2]
    width = features.shape[1]
    vert_count = lax.axis_size("vert")
    slot_count = send_list.shape[2]
    blocks = jnp.transpose(features.reshape(block_count, edge, width), (0, 2, 1))
    chosen = jnp.take(blocks, send_list[0], axis=0)
    arrived = lax.all_to_all(chosen, "vert", split_axis=0, concat_axis=0, tiled=True)
    extended = jnp.concatenate(
        [blocks, arrived.reshape(vert_count * slot_count, width, edge)], axis=0
    )
    total = jnp.zeros((width, block_count, edge), jnp.float32)
    for tile_slot in range(tile_depth):
        total = add_tile(total, extended, tiles, tile_cols, tile_count, tile_slot)
    hidden = total.astype(jnp.bfloat16).reshape(width, block_count * edge)
    full_rows = lax.all_to_all(hidden, "feat", split_axis=1, concat_axis=0, tiled=True)
    mixed_rows = lax.dot_general(
        full_rows, weight, (((0,), (0,)), ((), ())), preferred_element_type=jnp.float32
    )
    return jnp.maximum(mixed_rows + bias, jnp.float32(0.0)).astype(jnp.bfloat16)


def solution(mesh):
    return jax.shard_map(
        per_device,
        mesh=mesh,
        in_specs=(
            P("vert", "feat"),
            P("vert", None, None, None),
            P("vert", None),
            P("vert"),
            P("vert", None, None),
            P(),
            P(),
        ),
        out_specs=P(("vert", "feat"), None),
        check_vma=False,
    )
```

profile of v0, /device:TPU:1, one launch (start us, length us, event | category | flops | bytes accessed | tf_op | source)
XLA Modules:
  0.0 102.2 jit_solution(15791302507142877693)
XLA Ops:
  0.0 0.7 compare_select_fusion
  0.7 0.7 compare_and_fusion.16
  1.5 0.1 copy.69
  1.6 0.1 reshape.199
  1.7 0.1 copy.68
  1.8 0.6 gather_fusion
  2.4 0.8 broadcast_select_fusion
  3.2 7.6 %all-to-all-start = ((bf16[16,4,16,128]{3,2,1,0:T(8,128)(2,1)}), bf16[16,4,16,128]{3,2,1,0:T(8,128)(2,1)S(1)}, u32[]{:S(2)}, u32[]{:S(2)}) async-start(bf16[16,4,16,128]{3,2,1,0:T(8,128)(2,1)} %broadcast_select_fusion), calls=%async_computation | async-start | bytes 524288 | tf_op jit(solution)/shard_map/all_to_all | solution.py:25
  10.8 1.1 %compare_and_fusion = (pred[64]{0:T(512)(128)(4,1)S(1)}, s32[64]{0:T(128)S(1)}, pred[64]{0:T(512)(128)(4,1)S(1)}, s32[64]{0:T(128)S(1)}, pred[64]{0:T(512)(128)(...) fusion(s32[64,16]{0,1:T(8,128)} %param.11), kind=kLoop, calls=%fused_computation.187 | loop fusion | flops 6144 | bytes 9216 | tf_op jit(solution)/shard_map/jit(_take)/and | solution.py:9
  12.0 0.7 broadcast_compare_fusion
  12.7 5.6 %all-to-all-done = bf16[16,4,16,128]{3,2,1,0:T(8,128)(2,1)S(1)} async-done(((bf16[16,4,16,128]{3,2,1,0:T(8,128)(2,1)}), bf16[16,4,16,128]{3,2,1,0:T(8,128)(2,1)S(1)}, u32[]{:S(2)}, u32[]{:S(2)}) %all-to-all-start) | async-done | bytes 262176 | tf_op jit(solution)/shard_map/all_to_all | solution.py:25
  18.3 1.3 %gather_fusion.1 = bf16[64,16,128]{2,1,0:T(8,128)(2,1)} fusion(bf16[128,16,128]{2,1,0:T(8,128)(2,1)S(1)} %pad_maximum_fusion, s32[1024]{0:T(1024)S(1)} %get-tuple-element.99), kind=kCustom, calls=%fused_computation.clone | custom fusion | bytes 524544 | tf_op jit(solution)/shard_map/jit(_take)/gather | solution.py:9
  19.6 1.3 %gather_fusion.2 = bf16[64,16,128]{2,1,0:T(8,128)(2,1)} fusion(bf16[128,16,128]{2,1,0:T(8,128)(2,1)S(1)} %pad_maximum_fusion, s32[1024]{0:T(1024)S(1)} %get-tuple-element.98), kind=kCustom, calls=%fused_computation.1.clone | custom fusion | bytes 524544 | tf_op jit(solution)/shard_map/jit(_take)/gather | solution.py:9
  21.0 1.3 %gather_fusion.3 = bf16[64,16,128]{2,1,0:T(8,128)(2,1)} fusion(bf16[128,16,128]{2,1,0:T(8,128)(2,1)S(1)} %pad_maximum_fusion, s32[1024]{0:T(1024)S(1)} %get-tuple-element.97), kind=kCustom, calls=%fused_computation.2.clone | custom fusion | bytes 524544 | tf_op jit(solution)/shard_map/jit(_take)/gather | solution.py:9
  22.3 1.3 %gather_fusion.4 = bf16[64,16,128]{2,1,0:T(8,128)(2,1)} fusion(bf16[128,16,128]{2,1,0:T(8,128)(2,1)S(1)} %pad_maximum_fusion, s32[1024]{0:T(1024)S(1)} %get-tuple-element.96), kind=kCustom, calls=%fused_computation.3.clone | custom fusion | bytes 524544 | tf_op jit(solution)/shard_map/jit(_take)/gather | solution.py:9
  23.6 1.3 %gather_fusion.5 = bf16[64,16,128]{2,1,0:T(8,128)(2,1)} fusion(bf16[128,16,128]{2,1,0:T(8,128)(2,1)S(1)} %pad_maximum_fusion, s32[1024]{0:T(1024)S(1)} %get-tuple-element.95), kind=kCustom, calls=%fused_computation.4.clone | custom fusion | bytes 524544 | tf_op jit(solution)/shard_map/jit(_take)/gather | solution.py:9
  25.0 1.3 %gather_fusion.6 = bf16[64,16,128]{2,1,0:T(8,128)(2,1)} fusion(bf16[128,16,128]{2,1,0:T(8,128)(2,1)S(1)} %pad_maximum_fusion, s32[1024]{0:T(1024)S(1)} %get-tuple-element.94), kind=kCustom, calls=%fused_computation.5.clone | custom fusion | bytes 524544 | tf_op jit(solution)/shard_map/jit(_take)/gather | solution.py:9
  26.3 0.6 gather_fusion.7
  26.9 0.6 gather_fusion.8
  27.6 0.6 gather_fusion.9
  28.2 0.6 gather_fusion.10
  28.8 0.6 gather_fusion.11
  29.5 0.6 gather_fusion.12
  30.1 0.6 gather_fusion.13
  30.7 0.6 gather_fusion.14
  31.4 0.6 gather_fusion.15
  32.0 0.6 gather_fusion.16
  32.6 3.0 %fusion.48 = f32[64,16,128]{2,1,0:T(8,128)S(1)} fusion(bf16[64,16,128,128]{3,2,1,0:T(8,128)(2,1)} %param.10, bf16[64,16,128]{2,1,0:T(8,128)(2,1)} %gather_fusion.1, pred[64]{0:T(512)(128)(4,1)S(1)} %get-tuple-element.64, pred[64]{0:T(512)(128)(4,1)S(1)} %get-tuple-element.82), kind=kOutput, calls=%fused_computation.65 | convolution fusion | flops 33816576 | bytes 2883712 | tf_op jit(solution)/shard_map/rcj,rij->cri/dot_general | solution.py:11
  35.6 2.9 %fusion.141 = f32[64,16,128]{2,1,0:T(8,128)S(1)} fusion(f32[64,16,128]{2,1,0:T(8,128)S(1)} %fusion.48, bf16[64,16,128,128]{3,2,1,0:T(8,128)(2,1)} %param.10, bf16[64,16,128]{2,1,0:T(8,128)(2,1)} %gather_fusion.2, pred[64]{0:T(512)(128)(4,1)S(1)} %get-tuple-element.62, pred[64]{0:T(512)(128)(4,1)S(1)} %get-tuple-element.81), kind=kOutput, calls=%fused_computation.96 | convolution fusion | flops 33947648 | bytes 3408000 | tf_op jit(solution)/shard_map/rcj,rij->cri/dot_general | solution.py:11
  38.6 2.9 %fusion.138 = f32[64,16,128]{2,1,0:T(8,128)S(1)} fusion(f32[64,16,128]{2,1,0:T(8,128)S(1)} %fusion.141, bf16[64,16,128,128]{3,2,1,0:T(8,128)(2,1)} %param.10, bf16[64,16,128]{2,1,0:T(8,128)(2,1)} %gather_fusion.3, pred[64]{0:T(512)(128)(4,1)S(1)} %get-tuple-element.60, pred[64]{0:T(512)(128)(4,1)S(1)} %get-tuple-element.80), kind=kOutput, calls=%fused_computation.95 | convolution fusion | flops 33947648 | bytes 3408000 | tf_op jit(solution)/shard_map/rcj,rij->cri/dot_general | solution.py:11
  41.5 2.9 %fusion.135 = f32[64,16,128]{2,1,0:T(8,128)S(1)} fusion(f32[64,16,128]{2,1,0:T(8,128)S(1)} %fusion.138, bf16[64,16,128,128]{3,2,1,0:T(8,128)(2,1)} %param.10, bf16[64,16,128]{2,1,0:T(8,128)(2,1)} %gather_fusion.4, pred[64]{0:T(512)(128)(4,1)S(1)} %get-tuple-element.58, pred[64]{0:T(512)(128)(4,1)S(1)} %get-tuple-element.79), kind=kOutput, calls=%fused_computation.94 | convolution fusion | flops 33947648 | bytes 3408000 | tf_op jit(solution)/shard_map/rcj,rij->cri/dot_general | solution.py:11
  44.4 2.9 %fusion.132 = f32[64,16,128]{2,1,0:T(8,128)S(1)} fusion(f32[64,16,128]{2,1,0:T(8,128)S(1)} %fusion.135, bf16[64,16,128,128]{3,2,1,0:T(8,128)(2,1)} %param.10, bf16[64,16,128]{2,1,0:T(8,128)(2,1)} %gather_fusion.5, pred[64]{0:T(512)(128)(4,1)S(1)} %get-tuple-element.56, pred[64]{0:T(512)(128)(4,1)S(1)} %get-tuple-element.78), kind=kOutput, calls=%fused_computation.93 | convolution fusion | flops 33947648 | bytes 3408000 | tf_op jit(solution)/shard_map/rcj,rij->cri/dot_general | solution.py:11
  47.4 2.9 %fusion.129 = f32[64,16,128]{2,1,0:T(8,128)S(1)} fusion(f32[64,16,128]{2,1,0:T(8,128)S(1)} %fusion.132, bf16[64,16,128,128]{3,2,1,0:T(8,128)(2,1)} %param.10, bf16[64,16,128]{2,1,0:T(8,128)(2,1)} %gather_fusion.6, pred[64]{0:T(512)(128)(4,1)S(1)} %get-tuple-element.54, pred[64]{0:T(512)(128)(4,1)S(1)} %get-tuple-element.77), kind=kOutput, calls=%fused_computation.92 | convolution fusion | flops 33947648 | bytes 3408000 | tf_op jit(solution)/shard_map/rcj,rij->cri/dot_general | solution.py:11
  50.3 2.9 %fusion.126 = f32[64,16,128]{2,1,0:T(8,128)S(1)} fusion(f32[64,16,128]{2,1,0:T(8,128)S(1)} %fusion.129, bf16[64,16,128,128]{3,2,1,0:T(8,128)(2,1)} %param.10, bf16[64,16,128]{2,1,0:T(8,128)(2,1)S(1)} %gather_fusion.7, pred[64]{0:T(512)(128)(4,1)S(1)} %get-tuple-element.52, pred[64]{0:T(512)(128)(4,1)S(1)} %get-tuple-element.76), kind=kOutput, calls=%fused_computation.91 | convolution fusion | flops 33947648 | bytes 3408000 | tf_op jit(solution)/shard_map/rcj,rij->cri/dot_general | solution.py:11
  53.2 2.8 %fusion.123 = f32[64,16,128]{2,1,0:T(8,128)S(1)} fusion(f32[64,16,128]{2,1,0:T(8,128)S(1)} %fusion.126, bf16[64,16,128,128]{3,2,1,0:T(8,128)(2,1)} %param.10, bf16[64,16,128]{2,1,0:T(8,128)(2,1)S(1)} %gather_fusion.8, pred[64]{0:T(512)(128)(4,1)S(1)} %get-tuple-element.50, pred[64]{0:T(512)(128)(4,1)S(1)} %get-tuple-element.75), kind=kOutput, calls=%fused_computation.90 | convolution fusion | flops 33947648 | bytes 3408000 | tf_op jit(solution)/shard_map/rcj,rij->cri/dot_general | solution.py:11
  56.0 2.8 %fusion.120 = f32[64,16,128]{2,1,0:T(8,128)S(1)} fusion(f32[64,16,128]{2,1,0:T(8,128)S(1)} %fusion.123, bf16[64,16,128,128]{3,2,1,0:T(8,128)(2,1)} %param.10, bf16[64,16,128]{2,1,0:T(8,128)(2,1)S(1)} %gather_fusion.9, pred[64]{0:T(512)(128)(4,1)S(1)} %get-tuple-element.48, pred[64]{0:T(512)(128)(4,1)S(1)} %get-tuple-element.74), kind=kOutput, calls=%fused_computation.89 | convolution fusion | flops 33947648 | bytes 3408000 | tf_op jit(solution)/shard_map/rcj,rij->cri/dot_general | solution.py:11
  58.9 2.8 %fusion.117 = f32[64,16,128]{2,1,0:T(8,128)S(1)} fusion(f32[64,16,128]{2,1,0:T(8,128)S(1)} %fusion.120, bf16[64,16,128,128]{3,2,1,0:T(8,128)(2,1)} %param.10, bf16[64,16,128]{2,1,0:T(8,128)(2,1)S(1)} %gather_fusion.10, pred[64]{0:T(512)(128)(4,1)S(1)} %get-tuple-element.46, pred[64]{0:T(512)(128)(4,1)S(1)} %get-tuple-element.73), kind=kOutput, calls=%fused_computation.88 | convolution fusion | flops 33947648 | bytes 3408000 | tf_op jit(solution)/shard_map/rcj,rij->cri/dot_general | solution.py:11
  61.7 2.8 %fusion.114 = f32[64,16,128]{2,1,0:T(8,128)S(1)} fusion(f32[64,16,128]{2,1,0:T(8,128)S(1)} %fusion.117, bf16[64,16,128,128]{3,2,1,0:T(8,128)(2,1)} %param.10, bf16[64,16,128]{2,1,0:T(8,128)(2,1)S(1)} %gather_fusion.11, pred[64]{0:T(512)(128)(4,1)S(1)} %get-tuple-element.44, pred[64]{0:T(512)(128)(4,1)S(1)} %get-tuple-element.72), kind=kOutput, calls=%fused_computation.87 | convolution fusion | flops 33947648 | bytes 3408000 | tf_op jit(solution)/shard_map/rcj,rij->cri/dot_general | solution.py:11
  64.6 2.8 %fusion.111 = f32[64,16,128]{2,1,0:T(8,128)S(1)} fusion(f32[64,16,128]{2,1,0:T(8,128)S(1)} %fusion.114, bf16[64,16,128,128]{3,2,1,0:T(8,128)(2,1)} %param.10, bf16[64,16,128]{2,1,0:T(8,128)(2,1)S(1)} %gather_fusion.12, pred[64]{0:T(512)(128)(4,1)S(1)} %get-tuple-element.42, pred[64]{0:T(512)(128)(4,1)S(1)} %get-tuple-element.71), kind=kOutput, calls=%fused_computation.86 | convolution fusion | flops 33947648 | bytes 3408000 | tf_op jit(solution)/shard_map/rcj,rij->cri/dot_general | solution.py:11
  67.4 2.8 %fusion.108 = f32[64,16,128]{2,1,0:T(8,128)S(1)} fusion(f32[64,16,128]{2,1,0:T(8,128)S(1)} %fusion.111, bf16[64,16,128,128]{3,2,1,0:T(8,128)(2,1)} %param.10, bf16[64,16,128]{2,1,0:T(8,128)(2,1)S(1)} %gather_fusion.13, pred[64]{0:T(512)(128)(4,1)S(1)} %get-tuple-element.40, pred[64]{0:T(512)(128)(4,1)S(1)} %get-tuple-element.70), kind=kOutput, calls=%fused_computation.85 | convolution fusion | flops 33947648 | bytes 3408000 | tf_op jit(solution)/shard_map/rcj,rij->cri/dot_general | solution.py:11
  70.3 3.0 %fusion.105 = f32[64,16,128]{2,1,0:T(8,128)S(1)} fusion(f32[64,16,128]{2,1,0:T(8,128)S(1)} %fusion.108, bf16[64,16,128,128]{3,2,1,0:T(8,128)(2,1)} %param.10, bf16[64,16,128]{2,1,0:T(8,128)(2,1)S(1)} %gather_fusion.14, pred[64]{0:T(512)(128)(4,1)S(1)} %get-tuple-element.38, pred[64]{0:T(512)(128)(4,1)S(1)} %get-tuple-element.69), kind=kOutput, calls=%fused_computation.84 | convolution fusion | flops 33947648 | bytes 3408000 | tf_op jit(solution)/shard_map/rcj,rij->cri/dot_general | solution.py:11
  73.3 2.8 %fusion.102 = f32[64,16,128]{2,1,0:T(8,128)S(1)} fusion(f32[64,16,128]{2,1,0:T(8,128)S(1)} %fusion.105, bf16[64,16,128,128]{3,2,1,0:T(8,128)(2,1)} %param.10, bf16[64,16,128]{2,1,0:T(8,128)(2,1)S(1)} %gather_fusion.15, pred[64]{0:T(512)(128)(4,1)S(1)} %get-tuple-element.66, pred[64]{0:T(512)(128)(4,1)S(1)} %get-tuple-element.83), kind=kOutput, calls=%fused_computation.83 | convolution fusion | flops 33947648 | bytes 3408000 | tf_op jit(solution)/shard_map/rcj,rij->cri/dot_general | solution.py:11
  76.1 2.8 %fusion.146 = bf16[16,64,128]{2,0,1:T(8,128)(2,1)S(1)} fusion(f32[64,16,128]{2,1,0:T(8,128)S(1)} %fusion.102, bf16[64,16,128,128]{3,2,1,0:T(8,128)(2,1)} %param.10, bf16[64,16,128]{2,1,0:T(8,128)(2,1)S(1)} %gather_fusion.16, pred[64]{0:T(512)(128)(4,1)S(1)} %get-tuple-element.6, pred[64]{0:T(512)(128)(4,1)S(1)} %get-tuple-element.68), kind=kOutput, calls=%fused_computation.100 | convolution fusion | flops 34078720 | bytes 3145856 | tf_op jit(solution)/shard_map/rcj,rij->cri/dot_general | solution.py:11
  79.0 0.1 copy.86
  79.1 0.2 all_to_all.18
  79.2 0.2 copy.87
  79.4 21.9 %all_to_all.24 = bf16[16,16,512]{2,0,1:T(8,128)(2,1)S(1)} all-to-all(bf16[16,16,512]{2,0,1:T(8,128)(2,1)S(1)} %copy.87), channel_id=1, replica_groups=mesh['vert'=16,'feat'=16] {'feat'}, dimensions={1} | all-to-all | bytes 524288 | tf_op jit(solution)/shard_map/all_to_all | solution.py:33
  101.3 1.0 fusion.145
  (17 shorter events, 0.2 us)
Async XLA Ops:
  0.0 1.4 %copy-start = (bf16[8192,16]{0,1:T(8,128)(2,1)S(1)}, bf16[8192,16]{0,1:T(8,128)(2,1)}, u32[]{:S(2)}) copy-start(bf16[8192,16]{0,1:T(8,128)(2,1)} %param.9) | copy-start | bytes 786436
  1.8 99.5 %copy-start.2 = (f32[256]{0:T(256)S(1)}, f32[256]{0:T(256)}, u32[]{:S(2)}) copy-start(f32[256]{0:T(256)} %param.15) | copy-start | bytes 3076
  3.2 15.0 %all-to-all-start = ((bf16[16,4,16,128]{3,2,1,0:T(8,128)(2,1)}), bf16[16,4,16,128]{3,2,1,0:T(8,128)(2,1)S(1)}, u32[]{:S(2)}, u32[]{:S(2)}) async-start(bf16[16,4,16,128]{3,2,1,0:T(8,128)(2,1)} %broadcast_select_fusion), calls=%async_computation | async-start | bytes 524288 | tf_op jit(solution)/shard_map/all_to_all | solution.py:25
  32.6 68.6 %copy-start.1 = (bf16[256,256]{1,0:T(8,128)(2,1)S(1)}, bf16[256,256]{1,0:T(8,128)(2,1)}, u32[]{:S(2)}) copy-start(bf16[256,256]{1,0:T(8,128)(2,1)} %param.14) | copy-start | bytes 393220
where the time goes:
time: 103 us; the launch traced here: 102 us
  matrix products  47.3 us (46%)
  blocking collectives  21.9 us (21%)
  local copies, waits for them, and re-layouts  15.7 us (15%)
  starting transfers between devices  7.57 us (7%)
  waiting for transfers between devices  5.56 us (5%)
  other arithmetic  4.13 us (4%)
    dot_general x16, matrix products, add_tile(): jnp.einsum('rcj,rij->cri', picked, tile_page, preferred_element_type=jnp....  46.3 us
    all_to_all x1, blocking collectives, per_device(): lax.all_to_all(hidden, 'feat', split_axis=1, concat_axis=0, tiled=True)  21.9 us
    gather x16, local copies, waits for them, and re-layouts, add_tile(): picked = jnp.take(extended, wanted, axis=0)  14.3 us
    all_to_all x1, starting transfers between devices, per_device(): lax.all_to_all(chosen, 'vert', split_axis=0, concat_axis=0, tiled=True)  7.57 us
    all_to_all x1, waiting for transfers between devices, per_device(): lax.all_to_all(chosen, 'vert', split_axis=0, concat_axis=0, tiled=True)  5.56 us
  transfers between devices with their start and end apart: 1, of which 1 were waited for; matrix products, arithmetic and copies ran while one was open for 2% of the time, Pallas kernels for 0%

commit v1 on v0

v1 whole, which is shorter than its diff:
```python
import jax
import jax.numpy as jnp
from jax import lax
from jax.experimental import pallas as pl
from jax.experimental.pallas import tpu as pltpu
from jax.sharding import PartitionSpec as P

MESH = pl.DeviceIdType.MESH
EDGE = 128
SIDE = 4
NT = (((1,), (1,)), ((), ()))
TN = (((0,), (0,)), ((), ()))


def farthest_first(length):
    return sorted(range(1, length), key=lambda d: (-min(d, length - d), d))


def plane_order(side):
    steps = [(a, b) for a in range(side) for b in range(side) if a or b]
    reach = lambda d: min(d, side - d)
    return sorted(steps, key=lambda ab: (-(reach(ab[0]) + reach(ab[1])), ab))


def kernel(
    x_hbm, tiles_hbm, cols, count, listed, w_ref, bias_ref, out_ref,
    x_own, own, ext, chosen, held, agg, recv,
    x_sem, tile_sem, near_sems, halo_send, halo_recv, fwd_send, fwd_recv, far_send, far_recv,
):
    slots, verts = listed.shape
    depth = cols.shape[0]
    blocks = cols.shape[1]
    chips = recv.shape[1]
    part = recv.shape[0]
    width = x_own.shape[0]
    v = lax.axis_index("vert")
    f = lax.axis_index("feat")
    core = f % 2
    chip = f // 2
    row, column = v // SIDE, v % SIDE
    sibling = chip * 2 + (1 - core)

    x_copy = pltpu.make_async_copy(x_hbm, x_own, x_sem)
    x_copy.start()

    vert_peers = []
    for a, b in plane_order(SIDE):
        vert_peers.append(((row + a) % SIDE) * SIDE + (column + b) % SIDE)
    feat_steps = farthest_first(chips)
    barrier = pltpu.get_barrier_semaphore()
    for peer in vert_peers:
        pl.semaphore_signal(barrier, inc=1, device_id=(peer, f), device_id_type=MESH)
    for d in feat_steps:
        other = ((chip + d) % chips) * 2 + core
        pl.semaphore_signal(barrier, inc=1, device_id=(v, other), device_id_type=MESH)
    pl.semaphore_signal(barrier, inc=1, device_id=(v, sibling), device_id_type=MESH)

    order = feat_steps + [0]
    tile_copies = []
    for d in order:
        first = ((chip + d) % chips) * 2 * part + core * part
        tile_copies.append(
            pltpu.make_async_copy(tiles_hbm.at[pl.ds(first, part)], held.at[d], tile_sem.at[d])
        )
    for copy in tile_copies:
        copy.start()

    x_copy.wait()
    mine = ext.at[core]
    for g in range(blocks):
        block = x_own[:, g * EDGE:(g + 1) * EDGE]
        own[g] = block
        mine[g] = block
    ext[0, blocks + verts * slots] = jnp.zeros((width, EDGE), ext.dtype)
    ext[1, blocks + verts * slots] = jnp.zeros((width, EDGE), ext.dtype)
    for u in range(verts):
        for s in range(slots):
            chosen[u, s] = own[listed[s, u]]
    for s in range(slots):
        mine[blocks + v * slots + s] = own[listed[s, v]]

    pl.semaphore_wait(barrier, len(vert_peers) + len(feat_steps) + 1)

    halo = []
    for j, peer in enumerate(vert_peers):
        copy = pltpu.make_async_remote_copy(
            src_ref=chosen.at[peer],
            dst_ref=ext.at[core, pl.ds(blocks + v * slots, slots)],
            send_sem=halo_send.at[j],
            recv_sem=halo_recv.at[j],
            device_id=(peer, f),
            device_id_type=MESH,
        )
        copy.start()
        halo.append(copy)
    near = pltpu.make_async_remote_copy(
        src_ref=ext.at[core, pl.ds(0, blocks)],
        dst_ref=ext.at[core, pl.ds(0, blocks)],
        send_sem=near_sems.at[0],
        recv_sem=near_sems.at[1],
        device_id=(v, sibling),
        device_id_type=MESH,
    )
    near.start()

    def forward(j, source):
        place = pl.ds(blocks + source * slots, slots)
        return pltpu.make_async_remote_copy(
            src_ref=ext.at[core, place],
            dst_ref=ext.at[core, place],
            send_sem=fwd_send.at[j],
            recv_sem=fwd_recv.at[j],
            device_id=(v, sibling),
            device_id_type=MESH,
        )

    fwd = [forward(len(vert_peers), v)]
    fwd[0].start()
    for j in reversed(range(len(vert_peers))):
        a, b = plane_order(SIDE)[j]
        source = ((row + SIDE - a) % SIDE) * SIDE + (column + SIDE - b) % SIDE
        halo[j].wait_recv()
        copy = forward(j, source)
        copy.start()
        fwd.append(copy)
    for copy in tile_copies:
        copy.wait()
    near.wait_recv()
    for copy in fwd:
        copy.wait_recv()

    def far(i, d):
        return pltpu.make_async_remote_copy(
            src_ref=agg.at[i, d],
            dst_ref=recv.at[i, chip],
            send_sem=far_send.at[i, d],
            recv_sem=far_recv.at[i, d],
            device_id=(v, ((chip + d) % chips) * 2 + core),
            device_id_type=MESH,
        )

    def quarter(i, carry):
        for d in order:
            r = ((chip + d) % chips) * 2 * part + core * part + i
            live = count[r]
            left = []
            for k in range(depth):
                at = jnp.where(k < live, cols[k, r], blocks + verts * slots)
                left.append(jnp.concatenate([ext[0, at], ext[1, at]], axis=0))
            right = [held[d, i, k] for k in range(depth)]
            total = lax.dot_general(
                jnp.concatenate(left, axis=1), jnp.concatenate(right, axis=1), NT,
                preferred_element_type=jnp.float32,
            )
            if d:
                agg[i, d] = total.astype(agg.dtype)
                far(i, d).start()
            else:
                recv[i, chip] = total.astype(recv.dtype)
        return carry

    lax.fori_loop(0, part, quarter, 0)

    def finish(i, carry):
        for d in feat_steps:
            far(i, d).wait_recv()
        hidden = recv[i].reshape(chips * recv.shape[2], EDGE)
        mixed = lax.dot_general(hidden, w_ref[...], TN, preferred_element_type=jnp.float32)
        place = pl.ds(pl.multiple_of(i * EDGE, EDGE), EDGE)
        out_ref[place, :] = jnp.maximum(mixed + bias_ref[...], 0.0).astype(out_ref.dtype)
        return carry

    lax.fori_loop(0, part, finish, 0)

    for copy in halo:
        copy.wait_send()
    near.wait_send()
    for copy in fwd:
        copy.wait_send()

    def drain(i, carry):
        for d in feat_steps:
            far(i, d).wait_send()
        return carry

    lax.fori_loop(0, part, drain, 0)


def per_device(features, tiles, tile_cols, tile_count, send_list, weight, bias):
    blocks, depth, edge, _ = tiles.shape
    width = features.shape[1]
    verts, slots = send_list.shape[1:]
    devices = lax.axis_size("feat")
    chips = devices // 2
    part = blocks // devices
    any_space = pl.BlockSpec(memory_space=pl.ANY)
    smem = pl.BlockSpec(memory_space=pltpu.SMEM)
    vmem = pl.BlockSpec(memory_space=pltpu.VMEM)
    dma = pltpu.SemaphoreType.DMA
    return pl.pallas_call(
        kernel,
        out_shape=jax.ShapeDtypeStruct((part * edge, weight.shape[1]), jnp.bfloat16),
        in_specs=[any_space, any_space, smem, smem, smem, vmem, vmem],
        out_specs=vmem,
        scratch_shapes=[
            pltpu.VMEM((width, blocks * edge), jnp.bfloat16),
            pltpu.VMEM((blocks, width, edge), jnp.bfloat16),
            pltpu.VMEM((2, blocks + verts * slots + 1, width, edge), jnp.bfloat16),
            pltpu.VMEM((verts, slots, width, edge), jnp.bfloat16),
            pltpu.VMEM((chips, part, depth, edge, edge), jnp.bfloat16),
            pltpu.VMEM((part, chips, 2 * width, edge), jnp.bfloat16),
            pltpu.VMEM((part, chips, 2 * width, edge), jnp.bfloat16),
            dma,
            dma((chips,)),
            dma((2,)),
            dma((verts - 1,)),
            dma((verts - 1,)),
            dma((verts,)),
            dma((verts,)),
            dma((part, chips)),
            dma((part, chips)),
        ],
        compiler_params=pltpu.CompilerParams(
            collective_id=0, has_side_effects=True, vmem_limit_bytes=60 * 1024 * 1024
        ),
    )(
        features.T, tiles, tile_cols.T, tile_count, send_list[0].T, weight, bias[None, :]
    )


def solution(mesh):
    return jax.shard_map(
        per_device,
        mesh=mesh,
        in_specs=(
            P("vert", "feat"),
            P("vert", None, None, None),
            P("vert", None),
            P("vert"),
            P("vert", None, None),
            P(),
            P(),
        ),
        out_specs=P(("vert", "feat"), None),
        check_vma=False,
    )
```

time: 103 us -> 36.3 us (0.35)
  matrix products: 47.3 us -> 0 us
  Pallas kernels: 0 us -> 34.5 us
  blocking collectives: 21.9 us -> 0 us
  local copies, waits for them, and re-layouts: 15.7 us -> 1.67 us
  starting transfers between devices: 7.57 us -> 0 us
  waiting for transfers between devices: 5.56 us -> 0 us
  other arithmetic: 4.13 us -> 0 us
    dot_general x17 -> x0, matrix products: 47.3 us -> none  [the longest x16 46.3 us: add_tile(): jnp.einsum('rcj,rij->cri', picked, tile_page, preferred_element_type=jnp....]
    pallas_call x0 -> x1, Pallas kernels: none -> 34.5 us  [per_device(): pl.pallas_call(kernel, out_shape=jax.ShapeDtypeStruct((part * edge, weigh...]
    all_to_all x1 -> x0, blocking collectives: 21.9 us -> none  [per_device(): lax.all_to_all(hidden, 'feat', split_axis=1, concat_axis=0, tiled=True)]
    gather x17 -> x0, local copies, waits for them, and re-layouts: 14.9 us -> none  [the longest x16 14.3 us: add_tile(): picked = jnp.take(extended, wanted, axis=0)]
    all_to_all x1 -> x0, starting transfers between devices: 7.57 us -> none  [per_device(): lax.all_to_all(chosen, 'vert', split_axis=0, concat_axis=0, tiled=True)]
    all_to_all x1 -> x0, waiting for transfers between devices: 5.56 us -> none  [per_device(): lax.all_to_all(chosen, 'vert', split_axis=0, concat_axis=0, tiled=True)]
    and x2 -> x0, other arithmetic: 1.78 us -> none  [the longest x1 1.1 us: add_tile(): picked = jnp.take(extended, wanted, axis=0)]
    unnamed x6 -> x1, local copies, waits for them, and re-layouts: 0.01 us -> 1.67 us
  transfers between devices with their start and end apart: 1 -> 0, of which waited for: 1 -> 0; matrix products, arithmetic and copies ran while one was open for 2% -> 0% of each run, Pallas kernels for 0% -> 0%
where the time goes in v1:
time: 36.3 us; the launch traced here: 36.2 us
  Pallas kernels  34.5 us (95%)
  local copies, waits for them, and re-layouts  1.67 us (5%)
    pallas_call x1, Pallas kernels, per_device(): pl.pallas_call(kernel, out_shape=jax.ShapeDtypeStruct((part * edge, weigh...  34.5 us
    unnamed x1, local copies, waits for them, and re-layouts  1.67 us

profile of v1, /device:TPU:1, one launch (start us, length us, event | category | flops | bytes accessed | tf_op | source)
XLA Modules:
  0.0 36.2 jit_solution(12635259204313959406)
XLA Ops:
  0.0 34.5 %shard_map.73 = bf16[512,256]{1,0:T(8,128)(2,1)} custom-call(bf16[16,8192]{1,0:T(8,128)(2,1)} %bitcast.6, bf16[64,16,128,128]{3,2,1,0:T(8,128)(2,1)} %tiles_hbm.1, s32[16,64]{1,0:T(8,128)} %bitcast.7, s32[64]{0:T(128)} %count.1, s32[4,16]{1,0:T(4,128)} %bitcast.8, bf16[256,256]{1,0:T(8,128)(2,1)} %w_ref.1, f32[1,256]{1,0:T(1,128)} %bitcast.9), custom_call_target="tpu_custom_call" | custom-call | tf_op jit(solution)/shard_map/pallas_call | solution.py:200
  34.6 1.7 %copy.9 = bf16[512,256]{1,0:T(8,128)(2,1)} copy(bf16[512,256]{1,0:T(8,128)(2,1)} %shard_map.73) | data formatting | bytes 524288

commit v2 on v1

--- a/solution.py
+++ b/solution.py
@@ -23,9 +23,9 @@
 
 
 def kernel(
-    x_hbm, tiles_hbm, cols, count, listed, w_ref, bias_ref, out_ref,
-    x_own, own, ext, chosen, held, agg, recv,
-    x_sem, tile_sem, near_sems, halo_send, halo_recv, fwd_send, fwd_recv, far_send, far_recv,
+    x_hbm, tiles_hbm, cols_hbm, count_hbm, listed_hbm, w_hbm, bias_hbm, out_ref,
+    x_own, own, ext, chosen, held, agg, recv, cols, count, listed, w_ref, bias_ref,
+    load_sems, tile_sem, known, near_sems, halo_send, halo_recv, fwd_send, fwd_recv, far_send, far_recv,
 ):
     slots, verts = listed.shape
     depth = cols.shape[0]
@@ -40,20 +40,27 @@
     row, column = v // SIDE, v % SIDE
     sibling = chip * 2 + (1 - core)
 
-    x_copy = pltpu.make_async_copy(x_hbm, x_own, x_sem)
-    x_copy.start()
-
     vert_peers = []
     for a, b in plane_order(SIDE):
         vert_peers.append(((row + a) % SIDE) * SIDE + (column + b) % SIDE)
     feat_steps = farthest_first(chips)
     barrier = pltpu.get_barrier_semaphore()
     for peer in vert_peers:
-        pl.semaphore_signal(barrier, inc=1, device_id=(peer, f), device_id_type=MESH)
+        pl.semaphore_signal(barrier, inc=1, device_id=(peer, chip * 2), device_id_type=MESH)
     for d in feat_steps:
-        other = ((chip + d) % chips) * 2 + core
+        other = ((chip + d) % chips) * 2 + 1
         pl.semaphore_signal(barrier, inc=1, device_id=(v, other), device_id_type=MESH)
-    pl.semaphore_signal(barrier, inc=1, device_id=(v, sibling), device_id_type=MESH)
+
+    @pl.when(core == 1)
+    def _():
+        pl.semaphore_signal(barrier, inc=1, device_id=(v, sibling), device_id_type=MESH)
+
+    loads = []
+    for j, (source, target) in enumerate((
+        (x_hbm, x_own), (listed_hbm, listed), (cols_hbm, cols), (count_hbm, count), (w_hbm, w_ref), (bias_hbm, bias_ref),
+    )):
+        loads.append(pltpu.make_async_copy(source, target, load_sems.at[j]))
+        loads[-1].start()
 
     order = feat_steps + [0]
     tile_copies = []
@@ -65,7 +72,8 @@
     for copy in tile_copies:
         copy.start()
 
-    x_copy.wait()
+    loads[0].wait()
+    loads[1].wait()
     mine = ext.at[core]
     for g in range(blocks):
         block = x_own[:, g * EDGE:(g + 1) * EDGE]
@@ -79,7 +87,14 @@
     for s in range(slots):
         mine[blocks + v * slots + s] = own[listed[s, v]]
 
-    pl.semaphore_wait(barrier, len(vert_peers) + len(feat_steps) + 1)
+    @pl.when(core == 0)
+    def _():
+        pl.semaphore_wait(barrier, 2 * len(vert_peers) + 1)
+        pl.semaphore_signal(known, inc=1, device_id=(v, sibling), device_id_type=MESH)
+
+    @pl.when(core == 1)
+    def _():
+        pl.semaphore_wait(known, 1)
 
     halo = []
     for j, peer in enumerate(vert_peers):
@@ -123,7 +138,17 @@
         copy = forward(j, source)
         copy.start()
         fwd.append(copy)
-    for copy in tile_copies:
+
+    @pl.when(core == 1)
+    def _():
+        pl.semaphore_wait(barrier, 2 * len(feat_steps))
+        pl.semaphore_signal(known, inc=1, device_id=(v, sibling), device_id_type=MESH)
+
+    @pl.when(core == 0)
+    def _():
+        pl.semaphore_wait(known, 1)
+
+    for copy in loads[2:] + tile_copies:
         copy.wait()
     near.wait_recv()
     for copy in fwd:
@@ -193,14 +218,13 @@
     devices = lax.axis_size("feat")
     chips = devices // 2
     part = blocks // devices
-    any_space = pl.BlockSpec(memory_space=pl.ANY)
-    smem = pl.BlockSpec(memory_space=pltpu.SMEM)
+    hbm = pl.BlockSpec(memory_space=pltpu.HBM)
     vmem = pl.BlockSpec(memory_space=pltpu.VMEM)
     dma = pltpu.SemaphoreType.DMA
     return pl.pallas_call(
         kernel,
         out_shape=jax.ShapeDtypeStruct((part * edge, weight.shape[1]), jnp.bfloat16),
-        in_specs=[any_space, any_space, smem, smem, smem, vmem, vmem],
+        in_specs=[hbm] * 7,
         out_specs=vmem,
         scratch_shapes=[
             pltpu.VMEM((width, blocks * edge), jnp.bfloat16),
@@ -210,8 +234,14 @@
             pltpu.VMEM((chips, part, depth, edge, edge), jnp.bfloat16),
             pltpu.VMEM((part, chips, 2 * width, edge), jnp.bfloat16),
             pltpu.VMEM((part, chips, 2 * width, edge), jnp.bfloat16),
-            dma,
+            pltpu.SMEM((depth, blocks), jnp.int32),
+            pltpu.SMEM((blocks,), jnp.int32),
+            pltpu.SMEM((slots, verts), jnp.int32),
+            pltpu.VMEM(weight.shape, weight.dtype),
+            pltpu.VMEM((1, weight.shape[1]), bias.dtype),
+            dma((6,)),
             dma((chips,)),
+            pltpu.SemaphoreType.REGULAR,
             dma((2,)),
             dma((verts - 1,)),
             dma((verts - 1,)),
@@ -221,11 +251,12 @@
             dma((part, chips)),
         ],
         compiler_params=pltpu.CompilerParams(
-            collective_id=0, has_side_effects=True, vmem_limit_bytes=60 * 1024 * 1024
+            collective_id=0, has_side_effects=True, vmem_limit_bytes=28 * 1024 * 1024
         ),
-    )(
-        features.T, tiles, tile_cols.T, tile_count, send_list[0].T, weight, bias[None, :]
-    )
+    )(*(
+        pltpu.with_memory_space_constraint(operand, pltpu.HBM)
+        for operand in (features.T, tiles, tile_cols.T, tile_count, send_list[0].T, weight, bias[None, :])
+    ))
 
 
 def solution(mesh):

time: 36.3 us -> 34.8 us (0.959)
  local copies, waits for them, and re-layouts: 1.67 us -> 0.71 us
  Pallas kernels: 34.5 us -> 34 us
    unnamed x1, local copies, waits for them, and re-layouts: 1.67 us -> 0.71 us
    pallas_call x1, Pallas kernels: 34.5 us -> 34 us  [per_device(): pl.pallas_call(kernel, out_shape=jax.ShapeDtypeStruct((part * edge, weigh...]
where the time goes in v2:
time: 34.8 us
  Pallas kernels  34 us (98%)
  local copies, waits for them, and re-layouts  0.71 us (2%)
    pallas_call x1, Pallas kernels, per_device(): pl.pallas_call(kernel, out_shape=jax.ShapeDtypeStruct((part * edge, weigh...  34 us
    unnamed x1, local copies, waits for them, and re-layouts  0.71 us

profile of v2, /device:TPU:1, one launch (start us, length us, event | category | flops | bytes accessed | tf_op | source)
XLA Modules:
  0.0 34.8 jit_solution(15639563684491214887)
XLA Ops:
  0.0 34.0 %shard_map.73 = bf16[512,256]{1,0:T(8,128)(2,1)S(1)} custom-call(bf16[16,8192]{1,0:T(8,128)(2,1)} %bitcast.6, bf16[64,16,128,128]{3,2,1,0:T(8,128)(2,1)} %tiles_hbm.1, s32[16,64]{1,0:T(8,128)} %bitcast.7, s32[64]{0:T(128)} %count_hbm.1, s32[4,16]{1,0:T(4,128)} %bitcast.8, bf16[256,256]{1,0:T(8,128)(2,1)} %w_hbm.1, f32[1,256]{1,0:T(1,128)} %bitcast.9), custom_call_target="tpu_custom_call" | custom-call | tf_op jit(solution)/shard_map/pallas_call | solution.py:224
  34.0 0.7 %copy.9 = bf16[512,256]{1,0:T(8,128)(2,1)} copy(bf16[512,256]{1,0:T(8,128)(2,1)S(1)} %shard_map.73) | data formatting | bytes 524288

commit v3 on v2

--- a/solution.py
+++ b/solution.py
@@ -8,7 +8,6 @@
 MESH = pl.DeviceIdType.MESH
 EDGE = 128
 SIDE = 4
-NT = (((1,), (1,)), ((), ()))
 TN = (((0,), (0,)), ((), ()))
 
 
@@ -30,8 +29,7 @@
     slots, verts = listed.shape
     depth = cols.shape[0]
     blocks = cols.shape[1]
-    chips = recv.shape[1]
-    part = recv.shape[0]
+    chips, part = recv.shape[:2]
     width = x_own.shape[0]
     v = lax.axis_index("vert")
     f = lax.axis_index("feat")
@@ -62,14 +60,13 @@
         loads.append(pltpu.make_async_copy(source, target, load_sems.at[j]))
         loads[-1].start()
 
-    order = feat_steps + [0]
+    half = chips // 2
     tile_copies = []
-    for d in order:
-        first = ((chip + d) % chips) * 2 * part + core * part
-        tile_copies.append(
-            pltpu.make_async_copy(tiles_hbm.at[pl.ds(first, part)], held.at[d], tile_sem.at[d])
-        )
-    for copy in tile_copies:
+    for t in range(half):
+        for d in (half + t, half - 1 - t):
+            first = ((chip + d) % chips) * 2 * part + core * part
+            tile_copies.append((d, pltpu.make_async_copy(tiles_hbm.at[pl.ds(first, part)], held.at[d], tile_sem.at[d])))
+    for _, copy in tile_copies:
         copy.start()
 
     loads[0].wait()
@@ -129,6 +126,15 @@
             device_id_type=MESH,
         )
 
+    def turn(i, carry):
+        for k in range(depth):
+            held[carry, i, k] = held[carry, i, k].T
+        return carry
+
+    for d, copy in tile_copies:
+        copy.wait()
+        lax.fori_loop(0, part, turn, d)
+
     fwd = [forward(len(vert_peers), v)]
     fwd[0].start()
     for j in reversed(range(len(vert_peers))):
@@ -148,48 +154,51 @@
     def _():
         pl.semaphore_wait(known, 1)
 
-    for copy in loads[2:] + tile_copies:
+    for copy in loads[2:]:
         copy.wait()
     near.wait_recv()
     for copy in fwd:
         copy.wait_recv()
 
-    def far(i, d):
+    def far(d):
         return pltpu.make_async_remote_copy(
-            src_ref=agg.at[i, d],
-            dst_ref=recv.at[i, chip],
-            send_sem=far_send.at[i, d],
-            recv_sem=far_recv.at[i, d],
+            src_ref=agg.at[d],
+            dst_ref=recv.at[chip],
+            send_sem=far_send.at[d],
+            recv_sem=far_recv.at[d],
             device_id=(v, ((chip + d) % chips) * 2 + core),
             device_id_type=MESH,
         )
 
-    def quarter(i, carry):
-        for d in order:
-            r = ((chip + d) % chips) * 2 * part + core * part + i
-            live = count[r]
-            left = []
-            for k in range(depth):
-                at = jnp.where(k < live, cols[k, r], blocks + verts * slots)
-                left.append(jnp.concatenate([ext[0, at], ext[1, at]], axis=0))
-            right = [held[d, i, k] for k in range(depth)]
-            total = lax.dot_general(
-                jnp.concatenate(left, axis=1), jnp.concatenate(right, axis=1), NT,
-                preferred_element_type=jnp.float32,
-            )
-            if d:
-                agg[i, d] = total.astype(agg.dtype)
-                far(i, d).start()
-            else:
-                recv[i, chip] = total.astype(recv.dtype)
+    def stage(t, carry):
+        for d in (half + t, half - 1 - t):
+            for i in range(part):
+                r = ((chip + d) % chips) * 2 * part + core * part + i
+                live = count[r]
+                left = []
+                for k in range(depth):
+                    at = jnp.where(k < live, cols[k, r], blocks + verts * slots)
+                    left.append(jnp.concatenate([ext[0, at], ext[1, at]], axis=0))
+                total = jnp.dot(
+                    jnp.concatenate(left, axis=1), held[d, i].reshape(depth * EDGE, EDGE),
+                    preferred_element_type=jnp.float32,
+                )
+                agg[d, i] = total.astype(agg.dtype)
+        far(half + t).start()
+
+        @pl.when(t < half - 1)
+        def _():
+            far(half - 1 - t).start()
+
         return carry
 
-    lax.fori_loop(0, part, quarter, 0)
+    lax.fori_loop(0, half, stage, 0)
+    recv[chip] = agg[0]
+    for d in feat_steps:
+        far(d).wait_recv()
 
     def finish(i, carry):
-        for d in feat_steps:
-            far(i, d).wait_recv()
-        hidden = recv[i].reshape(chips * recv.shape[2], EDGE)
+        hidden = recv[:, i].reshape(chips * recv.shape[2], EDGE)
         mixed = lax.dot_general(hidden, w_ref[...], TN, preferred_element_type=jnp.float32)
         place = pl.ds(pl.multiple_of(i * EDGE, EDGE), EDGE)
         out_ref[place, :] = jnp.maximum(mixed + bias_ref[...], 0.0).astype(out_ref.dtype)
@@ -203,12 +212,8 @@
     for copy in fwd:
         copy.wait_send()
 
-    def drain(i, carry):
-        for d in feat_steps:
-            far(i, d).wait_send()
-        return carry
-
-    lax.fori_loop(0, part, drain, 0)
+    for d in feat_steps:
+        far(d).wait_send()
 
 
 def per_device(features, tiles, tile_cols, tile_count, send_list, weight, bias):
@@ -232,8 +237,8 @@
             pltpu.VMEM((2, blocks + verts * slots + 1, width, edge), jnp.bfloat16),
             pltpu.VMEM((verts, slots, width, edge), jnp.bfloat16),
             pltpu.VMEM((chips, part, depth, edge, edge), jnp.bfloat16),
-            pltpu.VMEM((part, chips, 2 * width, edge), jnp.bfloat16),
-            pltpu.VMEM((part, chips, 2 * width, edge), jnp.bfloat16),
+            pltpu.VMEM((chips, part, 2 * width, edge), jnp.bfloat16),
+            pltpu.VMEM((chips, part, 2 * width, edge), jnp.bfloat16),
             pltpu.SMEM((depth, blocks), jnp.int32),
             pltpu.SMEM((blocks,), jnp.int32),
             pltpu.SMEM((slots, verts), jnp.int32),
@@ -247,8 +252,8 @@
             dma((verts - 1,)),
             dma((verts,)),
             dma((verts,)),
-            dma((part, chips)),
-            dma((part, chips)),
+            dma((chips,)),
+            dma((chips,)),
         ],
         compiler_params=pltpu.CompilerParams(
             collective_id=0, has_side_effects=True, vmem_limit_bytes=28 * 1024 * 1024

time: 34.8 us -> 29 us (0.83)
  Pallas kernels: 34 us -> 28.3 us
    pallas_call x1, Pallas kernels: 34 us -> 28.3 us  [per_device(): pl.pallas_call(kernel, out_shape=jax.ShapeDtypeStruct((part * edge, weigh...]
where the time goes in v3:
time: 29 us
  Pallas kernels  28.3 us (98%)
  local copies, waits for them, and re-layouts  0.71 us (2%)
    pallas_call x1, Pallas kernels, per_device(): pl.pallas_call(kernel, out_shape=jax.ShapeDtypeStruct((part * edge, weigh...  28.3 us
    unnamed x1, local copies, waits for them, and re-layouts  0.71 us

profile of v3, /device:TPU:1, one launch (start us, length us, event | category | flops | bytes accessed | tf_op | source)
XLA Modules:
  0.0 29.0 jit_solution(17964561119794164163)
XLA Ops:
  0.0 28.3 %shard_map.73 = bf16[512,256]{1,0:T(8,128)(2,1)S(1)} custom-call(bf16[16,8192]{1,0:T(8,128)(2,1)} %bitcast.6, bf16[64,16,128,128]{3,2,1,0:T(8,128)(2,1)} %tiles_hbm.1, s32[16,64]{1,0:T(8,128)} %bitcast.7, s32[64]{0:T(128)} %count_hbm.1, s32[4,16]{1,0:T(4,128)} %bitcast.8, bf16[256,256]{1,0:T(8,128)(2,1)} %w_hbm.1, f32[1,256]{1,0:T(1,128)} %bitcast.9), custom_call_target="tpu_custom_call" | custom-call | tf_op jit(solution)/shard_map/pallas_call | solution.py:229
  28.3 0.7 %copy.9 = bf16[512,256]{1,0:T(8,128)(2,1)} copy(bf16[512,256]{1,0:T(8,128)(2,1)S(1)} %shard_map.73) | data formatting | bytes 524288

commit v4 on v3

--- a/solution.py
+++ b/solution.py
@@ -13,6 +13,11 @@
 
 def farthest_first(length):
     return sorted(range(1, length), key=lambda d: (-min(d, length - d), d))
+
+
+def hops(device):
+    row, column = device // SIDE, device % SIDE
+    return min(row, SIDE - row) + min(column, SIDE - column)
 
 
 def plane_order(side):
@@ -36,16 +41,15 @@
     core = f % 2
     chip = f // 2
     row, column = v // SIDE, v % SIDE
-    sibling = chip * 2 + (1 - core)
-
-    vert_peers = []
+    cross = 1 - core
+    sibling = chip * 2 + cross
+
+    vert_order = sorted(range(verts), key=hops)
+    barrier = pltpu.get_barrier_semaphore()
     for a, b in plane_order(SIDE):
-        vert_peers.append(((row + a) % SIDE) * SIDE + (column + b) % SIDE)
-    feat_steps = farthest_first(chips)
-    barrier = pltpu.get_barrier_semaphore()
-    for peer in vert_peers:
+        peer = ((row + a) % SIDE) * SIDE + (column + b) % SIDE
         pl.semaphore_signal(barrier, inc=1, device_id=(peer, chip * 2), device_id_type=MESH)
-    for d in feat_steps:
+    for d in farthest_first(chips):
         other = ((chip + d) % chips) * 2 + 1
         pl.semaphore_signal(barrier, inc=1, device_id=(v, other), device_id_type=MESH)
 
@@ -60,12 +64,10 @@
         loads.append(pltpu.make_async_copy(source, target, load_sems.at[j]))
         loads[-1].start()
 
-    half = chips // 2
     tile_copies = []
-    for t in range(half):
-        for d in (half + t, half - 1 - t):
-            first = ((chip + d) % chips) * 2 * part + core * part
-            tile_copies.append((d, pltpu.make_async_copy(tiles_hbm.at[pl.ds(first, part)], held.at[d], tile_sem.at[d])))
+    for z in range(chips):
+        first = z * 2 * part + core * part
+        tile_copies.append((z, pltpu.make_async_copy(tiles_hbm.at[pl.ds(first, part)], held.at[z], tile_sem.at[z])))
     for _, copy in tile_copies:
         copy.start()
 
@@ -86,25 +88,32 @@
 
     @pl.when(core == 0)
     def _():
-        pl.semaphore_wait(barrier, 2 * len(vert_peers) + 1)
+        pl.semaphore_wait(barrier, 2 * (verts - 1) + 1)
         pl.semaphore_signal(known, inc=1, device_id=(v, sibling), device_id_type=MESH)
 
     @pl.when(core == 1)
     def _():
         pl.semaphore_wait(known, 1)
 
-    halo = []
-    for j, peer in enumerate(vert_peers):
-        copy = pltpu.make_async_remote_copy(
+    def halo(peer):
+        return pltpu.make_async_remote_copy(
             src_ref=chosen.at[peer],
             dst_ref=ext.at[core, pl.ds(blocks + v * slots, slots)],
-            send_sem=halo_send.at[j],
-            recv_sem=halo_recv.at[j],
-            device_id=(peer, f),
+            send_sem=halo_send.at[peer],
+            recv_sem=halo_recv.at[v],
+            device_id=(peer, sibling),
             device_id_type=MESH,
         )
-        copy.start()
-        halo.append(copy)
+
+    def arrived(source):
+        place = ext.at[cross, pl.ds(blocks + source * slots, slots)]
+        return pltpu.make_async_copy(place, place, halo_recv.at[source])
+
+    for peer in vert_order:
+        @pl.when(peer != v)
+        def _():
+            halo(peer).start()
+
     near = pltpu.make_async_remote_copy(
         src_ref=ext.at[core, pl.ds(0, blocks)],
         dst_ref=ext.at[core, pl.ds(0, blocks)],
@@ -115,13 +124,13 @@
     )
     near.start()
 
-    def forward(j, source):
+    def forward(source, side):
         place = pl.ds(blocks + source * slots, slots)
         return pltpu.make_async_remote_copy(
-            src_ref=ext.at[core, place],
-            dst_ref=ext.at[core, place],
-            send_sem=fwd_send.at[j],
-            recv_sem=fwd_recv.at[j],
+            src_ref=ext.at[side, place],
+            dst_ref=ext.at[side, place],
+            send_sem=fwd_send.at[source],
+            recv_sem=fwd_recv.at[source],
             device_id=(v, sibling),
             device_id_type=MESH,
         )
@@ -135,19 +144,16 @@
         copy.wait()
         lax.fori_loop(0, part, turn, d)
 
-    fwd = [forward(len(vert_peers), v)]
-    fwd[0].start()
-    for j in reversed(range(len(vert_peers))):
-        a, b = plane_order(SIDE)[j]
-        source = ((row + SIDE - a) % SIDE) * SIDE + (column + SIDE - b) % SIDE
-        halo[j].wait_recv()
-        copy = forward(j, source)
-        copy.start()
-        fwd.append(copy)
+    forward(v, core).start()
+    for source in vert_order:
+        @pl.when(source != v)
+        def _():
+            arrived(source).wait()
+            forward(source, cross).start()
 
     @pl.when(core == 1)
     def _():
-        pl.semaphore_wait(barrier, 2 * len(feat_steps))
+        pl.semaphore_wait(barrier, 2 * (chips - 1))
         pl.semaphore_signal(known, inc=1, device_id=(v, sibling), device_id_type=MESH)
 
     @pl.when(core == 0)
@@ -157,63 +163,67 @@
     for copy in loads[2:]:
         copy.wait()
     near.wait_recv()
-    for copy in fwd:
-        copy.wait_recv()
-
-    def far(d):
+    for source in vert_order:
+        forward(source, cross).wait_recv()
+
+    def far(z, source):
         return pltpu.make_async_remote_copy(
-            src_ref=agg.at[d],
-            dst_ref=recv.at[chip],
-            send_sem=far_send.at[d],
-            recv_sem=far_recv.at[d],
-            device_id=(v, ((chip + d) % chips) * 2 + core),
+            src_ref=agg.at[z],
+            dst_ref=recv.at[source],
+            send_sem=far_send.at[z],
+            recv_sem=far_recv.at[source],
+            device_id=(v, z * 2 + core),
             device_id_type=MESH,
         )
 
-    def stage(t, carry):
-        for d in (half + t, half - 1 - t):
+    def stage(destinations):
+        for z in destinations:
             for i in range(part):
-                r = ((chip + d) % chips) * 2 * part + core * part + i
+                r = z * 2 * part + core * part + i
                 live = count[r]
                 left = []
                 for k in range(depth):
                     at = jnp.where(k < live, cols[k, r], blocks + verts * slots)
                     left.append(jnp.concatenate([ext[0, at], ext[1, at]], axis=0))
                 total = jnp.dot(
-                    jnp.concatenate(left, axis=1), held[d, i].reshape(depth * EDGE, EDGE),
+                    jnp.concatenate(left, axis=1), held[z, i].reshape(depth * EDGE, EDGE),
                     preferred_element_type=jnp.float32,
                 )
-                agg[d, i] = total.astype(agg.dtype)
-        far(half + t).start()
-
-        @pl.when(t < half - 1)
-        def _():
-            far(half - 1 - t).start()
-
+                agg[z, i] = total.astype(agg.dtype)
+        for z in destinations:
+            @pl.when(z != chip)
+            def _():
+                far(z, chip).start()
+
+    def pair(t, carry):
+        stage((2 * t + 1, 2 * t + 2))
         return carry
 
-    lax.fori_loop(0, half, stage, 0)
-    recv[chip] = agg[0]
-    for d in feat_steps:
-        far(d).wait_recv()
-
-    def finish(i, carry):
+    stage((0,))
+    lax.fori_loop(0, (chips - 2) // 2, pair, 0)
+    stage((chips - 1,))
+    recv[chip] = agg[chip]
+    for source in reversed(range(chips)):
+        @pl.when(source != chip)
+        def _():
+            far(source, source).wait_recv()
+
+    for i in range(part):
         hidden = recv[:, i].reshape(chips * recv.shape[2], EDGE)
         mixed = lax.dot_general(hidden, w_ref[...], TN, preferred_element_type=jnp.float32)
-        place = pl.ds(pl.multiple_of(i * EDGE, EDGE), EDGE)
-        out_ref[place, :] = jnp.maximum(mixed + bias_ref[...], 0.0).astype(out_ref.dtype)
-        return carry
-
-    lax.fori_loop(0, part, finish, 0)
-
-    for copy in halo:
-        copy.wait_send()
+        out_ref[i * EDGE:(i + 1) * EDGE, :] = jnp.maximum(mixed + bias_ref[...], 0.0).astype(out_ref.dtype)
+
     near.wait_send()
-    for copy in fwd:
-        copy.wait_send()
-
-    for d in feat_steps:
-        far(d).wait_send()
+    for u in range(verts):
+        @pl.when(u != v)
+        def _():
+            halo(u).wait_send()
+
+        forward(u, cross).wait_send()
+    for z in range(chips):
+        @pl.when(z != chip)
+        def _():
+            far(z, chip).wait_send()
 
 
 def per_device(features, tiles, tile_cols, tile_count, send_list, weight, bias):
@@ -248,8 +258,8 @@
             dma((chips,)),
             pltpu.SemaphoreType.REGULAR,
             dma((2,)),
-            dma((verts - 1,)),
-            dma((verts - 1,)),
+            dma((verts,)),
+            dma((verts,)),
             dma((verts,)),
             dma((verts,)),
             dma((chips,)),

time: 29 us -> 27.4 us (0.945)
  the two profiles are of different devices: /device:TPU:1 before, /device:TPU:32 now
where the time goes in v4:
time: 27.4 us; the launch traced here: 27.3 us
  Pallas kernels  26.6 us (97%)
  local copies, waits for them, and re-layouts  0.71 us (3%)
    pallas_call x1, Pallas kernels, per_device(): pl.pallas_call(kernel, out_shape=jax.ShapeDtypeStruct((part * edge, weigh...  26.6 us
    unnamed x1, local copies, waits for them, and re-layouts  0.71 us

profile of v4, /device:TPU:32, one launch (start us, length us, event | category | flops | bytes accessed | tf_op | source)
XLA Modules:
  0.0 27.3 jit_solution(8370624796573466191)
XLA Ops:
  0.0 26.6 %shard_map.73 = bf16[512,256]{1,0:T(8,128)(2,1)S(1)} custom-call(bf16[16,8192]{1,0:T(8,128)(2,1)} %bitcast.6, bf16[64,16,128,128]{3,2,1,0:T(8,128)(2,1)} %tiles_hbm.1, s32[16,64]{1,0:T(8,128)} %bitcast.7, s32[64]{0:T(128)} %count_hbm.1, s32[4,16]{1,0:T(4,128)} %bitcast.8, bf16[256,256]{1,0:T(8,128)(2,1)} %w_hbm.1, f32[1,256]{1,0:T(1,128)} %bitcast.9), custom_call_target="tpu_custom_call" | custom-call | tf_op jit(solution)/shard_map/pallas_call | solution.py:239
  26.6 0.7 %copy.9 = bf16[512,256]{1,0:T(8,128)(2,1)} copy(bf16[512,256]{1,0:T(8,128)(2,1)S(1)} %shard_map.73) | data formatting | bytes 524288

commit v5 on v4

--- a/solution.py
+++ b/solution.py
@@ -29,7 +29,7 @@
 def kernel(
     x_hbm, tiles_hbm, cols_hbm, count_hbm, listed_hbm, w_hbm, bias_hbm, out_ref,
     x_own, own, ext, chosen, held, agg, recv, cols, count, listed, w_ref, bias_ref,
-    load_sems, tile_sem, known, near_sems, halo_send, halo_recv, fwd_send, fwd_recv, far_send, far_recv,
+    load_sems, tile_sem, near_sems, halo_send, halo_recv, fwd_send, fwd_recv, far_send, far_recv,
 ):
     slots, verts = listed.shape
     depth = cols.shape[0]
@@ -48,14 +48,12 @@
     barrier = pltpu.get_barrier_semaphore()
     for a, b in plane_order(SIDE):
         peer = ((row + a) % SIDE) * SIDE + (column + b) % SIDE
-        pl.semaphore_signal(barrier, inc=1, device_id=(peer, chip * 2), device_id_type=MESH)
+        pl.semaphore_signal(barrier, inc=1, device_id=(peer, sibling), device_id_type=MESH)
     for d in farthest_first(chips):
-        other = ((chip + d) % chips) * 2 + 1
+        other = ((chip + d) % chips) * 2 + core
         pl.semaphore_signal(barrier, inc=1, device_id=(v, other), device_id_type=MESH)
 
-    @pl.when(core == 1)
-    def _():
-        pl.semaphore_signal(barrier, inc=1, device_id=(v, sibling), device_id_type=MESH)
+    pl.semaphore_signal(barrier, inc=1, device_id=(v, sibling), device_id_type=MESH)
 
     loads = []
     for j, (source, target) in enumerate((
@@ -86,14 +84,7 @@
     for s in range(slots):
         mine[blocks + v * slots + s] = own[listed[s, v]]
 
-    @pl.when(core == 0)
-    def _():
-        pl.semaphore_wait(barrier, 2 * (verts - 1) + 1)
-        pl.semaphore_signal(known, inc=1, device_id=(v, sibling), device_id_type=MESH)
-
-    @pl.when(core == 1)
-    def _():
-        pl.semaphore_wait(known, 1)
+    pl.semaphore_wait(barrier, verts + chips - 1)
 
     def halo(peer):
         return pltpu.make_async_remote_copy(
@@ -109,10 +100,8 @@
         place = ext.at[cross, pl.ds(blocks + source * slots, slots)]
         return pltpu.make_async_copy(place, place, halo_recv.at[source])
 
-    for peer in vert_order:
-        @pl.when(peer != v)
-        def _():
-            halo(peer).start()
+    for a, b in plane_order(SIDE):
+        halo(((row + a) % SIDE) * SIDE + (column + b) % SIDE).start()
 
     near = pltpu.make_async_remote_copy(
         src_ref=ext.at[core, pl.ds(0, blocks)],
@@ -150,15 +139,6 @@
         def _():
             arrived(source).wait()
             forward(source, cross).start()
-
-    @pl.when(core == 1)
-    def _():
-        pl.semaphore_wait(barrier, 2 * (chips - 1))
-        pl.semaphore_signal(known, inc=1, device_id=(v, sibling), device_id_type=MESH)
-
-    @pl.when(core == 0)
-    def _():
-        pl.semaphore_wait(known, 1)
 
     for copy in loads[2:]:
         copy.wait()
@@ -196,12 +176,13 @@
                 far(z, chip).start()
 
     def pair(t, carry):
-        stage((2 * t + 1, 2 * t + 2))
+        stage((2 * t + half, 2 * t + half + 1))
         return carry
 
-    stage((0,))
-    lax.fori_loop(0, (chips - 2) // 2, pair, 0)
-    stage((chips - 1,))
+    half = chips // 2
+    for z in range(half):
+        stage((z,))
+    lax.fori_loop(0, half // 2, pair, 0)
     recv[chip] = agg[chip]
     for source in reversed(range(chips)):
         @pl.when(source != chip)
@@ -256,7 +237,6 @@
             pltpu.VMEM((1, weight.shape[1]), bias.dtype),
             dma((6,)),
             dma((chips,)),
-            pltpu.SemaphoreType.REGULAR,
             dma((2,)),
             dma((verts,)),
             dma((verts,)),

time: 27.4 us -> 26.8 us (0.978)
  Pallas kernels: 26.6 us -> 26 us
    pallas_call x1, Pallas kernels: 26.6 us -> 26 us  [per_device(): pl.pallas_call(kernel, out_shape=jax.ShapeDtypeStruct((part * edge, weigh...]
where the time goes in v5:
time: 26.8 us; the launch traced here: 26.7 us
  Pallas kernels  26 us (97%)
  local copies, waits for them, and re-layouts  0.71 us (3%)
    pallas_call x1, Pallas kernels, per_device(): pl.pallas_call(kernel, out_shape=jax.ShapeDtypeStruct((part * edge, weigh...  26 us
    unnamed x1, local copies, waits for them, and re-layouts  0.71 us

profile of v5, /device:TPU:32, one launch (start us, length us, event | category | flops | bytes accessed | tf_op | source)
XLA Modules:
  0.0 26.7 jit_solution(12183471009901085857)
XLA Ops:
  0.0 26.0 %shard_map.73 = bf16[512,256]{1,0:T(8,128)(2,1)S(1)} custom-call(bf16[16,8192]{1,0:T(8,128)(2,1)} %bitcast.6, bf16[64,16,128,128]{3,2,1,0:T(8,128)(2,1)} %tiles_hbm.1, s32[16,64]{1,0:T(8,128)} %bitcast.7, s32[64]{0:T(128)} %count_hbm.1, s32[4,16]{1,0:T(4,128)} %bitcast.8, bf16[256,256]{1,0:T(8,128)(2,1)} %w_hbm.1, f32[1,256]{1,0:T(1,128)} %bitcast.9), custom_call_target="tpu_custom_call" | custom-call | tf_op jit(solution)/shard_map/pallas_call | solution.py:220
  26.0 0.7 %copy.9 = bf16[512,256]{1,0:T(8,128)(2,1)} copy(bf16[512,256]{1,0:T(8,128)(2,1)S(1)} %shard_map.73) | data formatting | bytes 524288
